TPU v7x, 32 devices: a whole 2x2x4 slice. The times are simulated.
32 devices in a mesh: job: 2 (over core), replica: 4 (over z), model: 4 (over y, x).
Axes of the slice: x: 2, y: 2, z: 4, core: 2. Of those that a mesh axis runs over, the one named last changes fastest.
Arguments:
- grad_query: float32 [8, 1024, 1024], P(('job', 'replica'), None, 'model'), parts along dimension 0, may hold values from -0.875 to 0.875
- grad_key: float32 [8, 1024, 1024], P(('job', 'replica'), None, 'model'), parts along dimension 0, may hold values from -0.875 to 0.875
- grad_value: float32 [8, 1024, 1024], P(('job', 'replica'), None, 'model'), parts along dimension 0, may hold values from -0.875 to 0.875
- grad_mixed: float32 [8, 1024, 1024], P(('job', 'replica'), 'model'), parts along dimension 0, may hold values from -0.875 to 0.875
- grad_norm: float32 [8, 1024], P(('job', 'replica')), parts along dimension 0, may hold values from -8 to 8
- weight_query: float32 [2048, 1024], P(('job', 'replica'), 'model'), parts along dimension 0, may hold values from -0.25 to 0.25
- weight_key: float32 [2048, 1024], P(('job', 'replica'), 'model'), parts along dimension 0, may hold values from -0.25 to 0.25
- weight_value: float32 [2048, 1024], P(('job', 'replica'), 'model'), parts along dimension 0, may hold values from -0.25 to 0.25
- weight_mixed: float32 [2048, 1024], P(('job', 'model'), 'replica'), parts along dimension 0, may hold values from -0.25 to 0.25
- weight_norm: float32 [2048], P(('job', 'replica')), parts along dimension 0, may hold values from 0.25 to 1.75
- moment_query: float32 [2048, 1024], P(('job', 'replica'), 'model'), parts along dimension 0, may hold values from -0.1875 to 0.1875
- moment_key: float32 [2048, 1024], P(('job', 'replica'), 'model'), parts along dimension 0, may hold values from -0.1875 to 0.1875
- moment_value: float32 [2048, 1024], P(('job', 'replica'), 'model'), parts along dimension 0, may hold values from -0.1875 to 0.1875
- moment_mixed: float32 [2048, 1024], P(('job', 'model'), 'replica'), parts along dimension 0, may hold values from -0.1875 to 0.1875
- moment_norm: float32 [2048], P(('job', 'replica')), parts along dimension 0, may hold values from -1.75 to 1.75
Outputs:
- copy_query: bfloat16 [2048, 1024], P('job', 'model'), parts along dimension 0
- copy_key: bfloat16 [2048, 1024], P('job', 'model'), parts along dimension 0
- copy_value: bfloat16 [2048, 1024], P('job', 'model'), parts along dimension 0
- copy_mixed: bfloat16 [2048, 1024], P(('job', 'model')), parts along dimension 0
- copy_norm: bfloat16 [2048], P('job'), parts along dimension 0
- new_query: float32 [2048, 1024], P(('job', 'replica'), 'model'), parts along dimension 0
- new_key: float32 [2048, 1024], P(('job', 'replica'), 'model'), parts along dimension 0
- new_value: float32 [2048, 1024], P(('job', 'replica'), 'model'), parts along dimension 0
- new_mixed: float32 [2048, 1024], P(('job', 'model'), 'replica'), parts along dimension 0
- new_norm: float32 [2048], P(('job', 'replica')), parts along dimension 0
- state_new_query: float32 [2048, 1024], P(('job', 'replica'), 'model'), parts along dimension 0
- state_new_key: float32 [2048, 1024], P(('job', 'replica'), 'model'), parts along dimension 0
- state_new_value: float32 [2048, 1024], P(('job', 'replica'), 'model'), parts along dimension 0
- state_new_mixed: float32 [2048, 1024], P(('job', 'model'), 'replica'), parts along dimension 0
- state_new_norm: float32 [2048], P(('job', 'replica')), parts along dimension 0
There are 2 independent parts, one for each index of `job`. A program takes and returns all parts, laid end to end along the dimension named above; each array names one. Nothing has to cross between parts.
All inputs are finite; a program needn't handle non-finite values.
Results may differ from a plain program's by a relative error of at most 0.0004.
Values may be sent and summed in bfloat16 or wider, within the bound.
No kernel may reach another device: no remote copies, remote signals or barrier semaphores. Data moves between devices by JAX's collectives and lax.ppermute only.
A program may use at most 64 MiB of HBM per device.

v0:
```python
import jax
import jax.numpy as jnp
from jax import lax
from jax.sharding import PartitionSpec as P

learn_rate = 0.5
hold_rate = 0.9


def local(
    grad_query,
    grad_key,
    grad_value,
    grad_mixed,
    grad_norm,
    weight_query,
    weight_key,
    weight_value,
    weight_mixed,
    weight_norm,
    moment_query,
    moment_key,
    moment_value,
    moment_mixed,
    moment_norm,
):
    mean_query, mean_key, mean_value, mean_mixed = (
        lax.psum_scatter(grad_query[0], "replica", scatter_dimension=0, tiled=True),
        lax.psum_scatter(grad_key[0], "replica", scatter_dimension=0, tiled=True),
        lax.psum_scatter(grad_value[0], "replica", scatter_dimension=0, tiled=True),
        lax.psum_scatter(grad_mixed[0], "replica", scatter_dimension=1, tiled=True),
    )
    whole_norm = lax.psum(grad_norm[0], "replica")
    place = lax.axis_index("replica")
    mean_norm = lax.dynamic_slice_in_dim(
        whole_norm, place * weight_norm.shape[0], weight_norm.shape[0]
    )
    mean_rate = lax.axis_size("replica") ** (-0.5)
    mean_query = mean_query * mean_rate
    mean_key = mean_key * mean_rate
    mean_value = mean_value * mean_rate
    mean_mixed = mean_mixed * mean_rate
    mean_norm = mean_norm * mean_rate
    (
        own_query,
        own_key,
        own_value,
        own_mixed,
        slope_query_norm,
        slope_key_norm,
        slope_value_norm,
        slope_mixed_norm,
    ) = lax.psum(
        (
            jnp.sum(weight_query * weight_query, axis=1, keepdims=True),
            jnp.sum(weight_key * weight_key, axis=1, keepdims=True),
            jnp.sum(weight_value * weight_value, axis=1, keepdims=True),
            jnp.sum(weight_mixed * weight_mixed, axis=0, keepdims=True),
            jnp.sum(mean_query * mean_query, axis=1, keepdims=True),
            jnp.sum(mean_key * mean_key, axis=1, keepdims=True),
            jnp.sum(mean_value * mean_value, axis=1, keepdims=True),
            jnp.sum(mean_mixed * mean_mixed, axis=0, keepdims=True),
        ),
        "model",
    )
    mean_query = mean_query * (jnp.sqrt(own_query) * lax.rsqrt(slope_query_norm + 1e-06))
    mean_key = mean_key * (jnp.sqrt(own_key) * lax.rsqrt(slope_key_norm + 1e-06))
    mean_value = mean_value * (jnp.sqrt(own_value) * lax.rsqrt(slope_value_norm + 1e-06))
    mean_mixed = mean_mixed * (jnp.sqrt(own_mixed) * lax.rsqrt(slope_mixed_norm + 1e-06))
    state_new_query = hold_rate * moment_query + mean_query
    new_query = weight_query - learn_rate * state_new_query
    state_new_key = hold_rate * moment_key + mean_key
    new_key = weight_key - learn_rate * state_new_key
    state_new_value = hold_rate * moment_value + mean_value
    new_value = weight_value - learn_rate * state_new_value
    state_new_mixed = hold_rate * moment_mixed + mean_mixed
    new_mixed = weight_mixed - learn_rate * state_new_mixed
    state_new_norm = hold_rate * moment_norm + mean_norm
    new_norm = weight_norm - learn_rate * state_new_norm
    copy_query, copy_key, copy_value, copy_mixed, copy_norm = (
        lax.all_gather(new_query.astype(jnp.bfloat16), "replica", axis=0, tiled=True),
        lax.all_gather(new_key.astype(jnp.bfloat16), "replica", axis=0, tiled=True),
        lax.all_gather(new_value.astype(jnp.bfloat16), "replica", axis=0, tiled=True),
        lax.all_gather(new_mixed.astype(jnp.bfloat16), "replica", axis=1, tiled=True),
        lax.all_gather(new_norm.astype(jnp.bfloat16), "replica", axis=0, tiled=True),
    )
    return (
        copy_query,
        copy_key,
        copy_value,
        copy_mixed,
        copy_norm,
        new_query,
        new_key,
        new_value,
        new_mixed,
        new_norm,
        state_new_query,
        state_new_key,
        state_new_value,
        state_new_mixed,
        state_new_norm,
    )


def solution(mesh):
    placed = (
        P(("job", "replica"), None, "model"),
        P(("job", "replica"), None, "model"),
        P(("job", "replica"), None, "model"),
        P(("job", "replica"), "model", None),
        P(("job", "replica"), None),
        P(("job", "replica"), "model"),
        P(("job", "replica"), "model"),
        P(("job", "replica"), "model"),
        P(("job", "model"), "replica"),
        P(("job", "replica")),
        P(("job", "replica"), "model"),
        P(("job", "replica"), "model"),
        P(("job", "replica"), "model"),
        P(("job", "model"), "replica"),
        P(("job", "replica")),
    )
    return jax.shard_map(
        local,
        mesh=mesh,
        in_specs=placed,
        out_specs=(
            P("job", "model"),
            P("job", "model"),
            P("job", "model"),
            P(("job", "model"), None),
            P("job"),
            P(("job", "replica"), "model"),
            P(("job", "replica"), "model"),
            P(("job", "replica"), "model"),
            P(("job", "model"), "replica"),
            P(("job", "replica")),
            P(("job", "replica"), "model"),
            P(("job", "replica"), "model"),
            P(("job", "replica"), "model"),
            P(("job", "model"), "replica"),
            P(("job", "replica")),
        ),
        check_vma=False,
    )
```

profile of v0, /device:TPU:0, one launch (start us, length us, event | category | flops | bytes accessed | tf_op | source)
XLA Modules:
  0.0 210.1 jit_solution(8399502176376450542)
XLA Ops:
  10.1 13.5 %psum.71 = f32[1024]{0:T(1024)S(1)} all-reduce(f32[1024]{0:T(1024)S(1)} %bitcast.36), channel_id=1, replica_groups=mesh['job'=2,'replica'=4,'model'=4] {'replica'}, use_global_device_ids=true, to_apply=%region_20.0 | all-reduce | flops 1024 | bytes 8192 | tf_op jit(solution)/shard_map/psum | solution.py:33
  24.3 7.7 %all-gather = bf16[4,1,256]{2,1,0:T(2,128)(2,1)S(1)} all-gather(bf16[1,1,256]{2,1,0:T(2,128)(2,1)S(1)} %reshape.38), channel_id=1, replica_groups=mesh['job'=2,'replica'=4,'model'=4] {'replica'}, dimensions={0}, use_global_device_ids=true | all-gather | bytes 2560 | tf_op jit(solution)/shard_map/all_gather | solution.py:85
  32.8 0.8 copy-done
  33.8 6.6 %reduce-scatter.9.cloned.1.call-done = f32[256,256]{1,0:T(8,128)} async-done(((f32[1024,256]{1,0:T(8,128)}), f32[256,256]{1,0:T(8,128)}) %reduce-scatter.9.cloned.1.call-update) | async-done | bytes 262160 | tf_op jit(solution)/shard_map/reduce_scatter | solution.py:30
  40.4 1.1 multiply_reduce_fusion.2
  41.5 27.1 %reduce-scatter.11.cloned.1.call-done = f32[256,256]{1,0:T(8,128)} async-done(((f32[256,1024]{1,0:T(8,128)}), f32[256,256]{1,0:T(8,128)}) %reduce-scatter.11.cloned.1.call-update) | async-done | bytes 262160 | tf_op jit(solution)/shard_map/reduce_scatter | solution.py:31
  68.6 1.0 multiply_reduce_fusion
  69.6 27.1 %reduce-scatter.5.cloned.1.call-done = f32[256,256]{1,0:T(8,128)} async-done(((f32[1024,256]{1,0:T(8,128)}), f32[256,256]{1,0:T(8,128)}) %reduce-scatter.5.cloned.1.call-update) | async-done | bytes 262160 | tf_op jit(solution)/shard_map/reduce_scatter | solution.py:28
  96.7 1.1 multiply_reduce_fusion.6
  97.7 26.9 %reduce-scatter.7.cloned.1.call-done = f32[256,256]{1,0:T(8,128)} async-done(((f32[1024,256]{1,0:T(8,128)}), f32[256,256]{1,0:T(8,128)}) %reduce-scatter.7.cloned.1.call-update) | async-done | bytes 262160 | tf_op jit(solution)/shard_map/reduce_scatter | solution.py:29
  124.7 1.1 multiply_reduce_fusion.4
  125.8 10.0 %all-reduce = (f32[256,1]{0,1:T(1,128)S(1)}, f32[256,1]{0,1:T(1,128)S(1)}, f32[256,1]{0,1:T(1,128)S(1)}, f32[256,1]{0,1:T(1,128)S(1)}, f32[256,1]{0,1:T(1,128)S(...) all-reduce(f32[256,1]{0,1:T(1,128)S(1)} %bitcast.34, ...), channel_id=1, replica_groups=mesh['job'=2,'replica'=4,'model'=4] {'model'}, use_global_device_ids=true, to_apply=%region_4.0 | all-reduce | flops 2048 | bytes 16384 | tf_op jit(solution)/shard_map/psum | solution.py:53
  135.8 0.9 fusion.3
  136.7 14.8 %all_gather.16 = bf16[1024,256]{1,0:T(8,128)(2,1)S(1)} all-gather(bf16[256,256]{1,0:T(8,128)(2,1)S(1)} %get-tuple-element.32), channel_id=1, replica_groups=mesh['job'=2,'replica'=4,'model'=4] {'replica'}, dimensions={0}, use_global_device_ids=true | all-gather | bytes 655360 | tf_op jit(solution)/shard_map/all_gather | solution.py:82
  151.5 0.9 fusion.2
  152.4 15.3 %all_gather.17 = bf16[1024,256]{1,0:T(8,128)(2,1)S(1)} all-gather(bf16[256,256]{1,0:T(8,128)(2,1)S(1)} %get-tuple-element.29), channel_id=1, replica_groups=mesh['job'=2,'replica'=4,'model'=4] {'replica'}, dimensions={0}, use_global_device_ids=true | all-gather | bytes 655360 | tf_op jit(solution)/shard_map/all_gather | solution.py:83
  167.8 0.8 fusion.1
  168.6 16.1 %all_gather.18 = bf16[256,1024]{1,0:T(8,128)(2,1)S(1)} all-gather(bf16[256,256]{1,0:T(8,128)(2,1)S(1)} %get-tuple-element.26), channel_id=1, replica_groups=mesh['job'=2,'replica'=4,'model'=4] {'replica'}, dimensions={1}, use_global_device_ids=true | all-gather | bytes 655360 | tf_op jit(solution)/shard_map/all_gather | solution.py:84
  184.7 0.9 fusion.4
  185.7 14.8 %all_gather.15 = bf16[1024,256]{1,0:T(8,128)(2,1)S(1)} all-gather(bf16[256,256]{1,0:T(8,128)(2,1)S(1)} %get-tuple-element.35), channel_id=1, replica_groups=mesh['job'=2,'replica'=4,'model'=4] {'replica'}, dimensions={0}, use_global_device_ids=true | all-gather | bytes 655360 | tf_op jit(solution)/shard_map/all_gather | solution.py:81
  200.4 0.8 copy.35
  201.2 0.8 copy.36
  202.0 0.8 copy.37
  202.8 0.8 copy.38
  (48 shorter events, 4.6 us)
Async XLA Ops:
  7.2 33.2 %reduce-scatter.9.cloned.1.call-start = ((), (), s32[]{:S(2)}) async-start(), calls=%async_computation.6 | async-start | bytes 1310720 | tf_op jit(solution)/shard_map/reduce_scatter | solution.py:30
  7.9 60.6 %reduce-scatter.11.cloned.1.call-start = ((), (), s32[]{:S(2)}) async-start(), calls=%async_computation.7 | async-start | bytes 1310720 | tf_op jit(solution)/shard_map/reduce_scatter | solution.py:31
  8.7 88.0 %reduce-scatter.5.cloned.1.call-start = ((), (), s32[]{:S(2)}) async-start(), calls=%async_computation.4 | async-start | bytes 1310720 | tf_op jit(solution)/shard_map/reduce_scatter | solution.py:28
  9.4 115.2 %reduce-scatter.7.cloned.1.call-start = ((), (), s32[]{:S(2)}) async-start(), calls=%async_computation.5 | async-start | bytes 1310720 | tf_op jit(solution)/shard_map/reduce_scatter | solution.py:29
  9.4 0.7 copy-start.12
  9.5 14.1 %copy-start.13 = (f32[256]{0:T(256)S(1)}, f32[256]{0:T(256)}, u32[]{:S(2)}) copy-start(f32[256]{0:T(256)} %param.24) | copy-start | bytes 3076
  9.5 14.1 %copy-start.14 = (f32[256]{0:T(256)S(1)}, f32[256]{0:T(256)}, u32[]{:S(2)}) copy-start(f32[256]{0:T(256)} %param.29) | copy-start | bytes 3076
  9.5 23.1 %copy-start.3 = (f32[256,256]{1,0:T(8,128)S(1)}, f32[256,256]{1,0:T(8,128)}, u32[]{:S(2)}) copy-start(f32[256,256]{1,0:T(8,128)} %param.20) | copy-start | bytes 786436
  10.0 22.7 %copy-start.2 = (f32[256,256]{1,0:T(8,128)S(1)}, f32[256,256]{1,0:T(8,128)}, u32[]{:S(2)}) copy-start(f32[256,256]{1,0:T(8,128)} %param.23) | copy-start | bytes 786436
  32.6 1.0 copy-start
  32.7 1.0 copy-start.1
  69.6 66.2 %copy-start.8 = (f32[256,256]{1,0:T(8,128)S(1)}, f32[256,256]{1,0:T(8,128)}, u32[]{:S(2)}) copy-start(f32[256,256]{1,0:T(8,128)} %param.26) | copy-start | bytes 786436
  124.7 11.2 %copy-start.7 = (f32[256,256]{1,0:T(8,128)S(1)}, f32[256,256]{1,0:T(8,128)}, u32[]{:S(2)}) copy-start(f32[256,256]{1,0:T(8,128)} %reduce-scatter.7.cloned.1.call-done) | copy-start | bytes 786436
  136.7 14.8 %copy-start.6 = (f32[256,256]{1,0:T(8,128)S(1)}, f32[256,256]{1,0:T(8,128)}, u32[]{:S(2)}) copy-start(f32[256,256]{1,0:T(8,128)} %reduce-scatter.9.cloned.1.call-done) | copy-start | bytes 786436
  136.7 14.8 %copy-start.9 = (f32[256,256]{1,0:T(8,128)S(1)}, f32[256,256]{1,0:T(8,128)}, u32[]{:S(2)}) copy-start(f32[256,256]{1,0:T(8,128)} %param.27) | copy-start | bytes 786436
  152.4 15.3 %copy-start.5 = (f32[256,256]{1,0:T(8,128)S(1)}, f32[256,256]{1,0:T(8,128)}, u32[]{:S(2)}) copy-start(f32[256,256]{1,0:T(8,128)} %reduce-scatter.11.cloned.1.call-done) | copy-start | bytes 786436
  152.4 15.4 %copy-start.10 = (f32[256,256]{1,0:T(8,128)S(1)}, f32[256,256]{1,0:T(8,128)}, u32[]{:S(2)}) copy-start(f32[256,256]{1,0:T(8,128)} %param.28) | copy-start | bytes 786436
  168.6 16.1 %copy-start.4 = (f32[256,256]{1,0:T(8,128)S(1)}, f32[256,256]{1,0:T(8,128)}, u32[]{:S(2)}) copy-start(f32[256,256]{1,0:T(8,128)} %reduce-scatter.5.cloned.1.call-done) | copy-start | bytes 786436
  168.6 16.1 %copy-start.11 = (f32[256,256]{1,0:T(8,128)S(1)}, f32[256,256]{1,0:T(8,128)}, u32[]{:S(2)}) copy-start(f32[256,256]{1,0:T(8,128)} %param.25) | copy-start | bytes 786436
Sparse Core Ops, SparseCore 0:
  10.3 30.1 reduce-scatter.8
  42.7 25.7 reduce-scatter.10
  70.9 25.7 reduce-scatter.4
  98.8 25.7 reduce-scatter.6
where the time goes:
time: 210 us
  blocking collectives  92.1 us (44%)
  waiting for transfers between devices  90.2 us (43%)
  between operations  14 us (7%)
  other arithmetic  8.91 us (4%)
  local copies, waits for them, and re-layouts  4.75 us (2%)
    reduce_scatter x1, waiting for transfers between devices, local(): lax.psum_scatter(grad_query[0], 'replica', scatter_dimension=0, tiled=True)  27.1 us
    reduce_scatter x1, waiting for transfers between devices, local(): lax.psum_scatter(grad_mixed[0], 'replica', scatter_dimension=1, tiled=True)  27.1 us
    reduce_scatter x1, waiting for transfers between devices, local(): lax.psum_scatter(grad_key[0], 'replica', scatter_dimension=0, tiled=True)  26.9 us
    all_gather x1, blocking collectives, local(): lax.all_gather(new_mixed.astype(jnp.bfloat16), 'replica', axis=1, tiled=T...  16.1 us
    all_gather x1, blocking collectives, local(): lax.all_gather(new_value.astype(jnp.bfloat16), 'replica', axis=0, tiled=T...  15.3 us
    all_gather x1, blocking collectives, local(): lax.all_gather(new_key.astype(jnp.bfloat16), 'replica', axis=0, tiled=True)  14.8 us
    all_gather x1, blocking collectives, local(): lax.all_gather(new_query.astype(jnp.bfloat16), 'replica', axis=0, tiled=T...  14.8 us
    psum x1, blocking collectives, local(): whole_norm = lax.psum(grad_norm[0], 'replica')  13.5 us
  transfers between devices with their start and end apart: 4, of which 4 were waited for; matrix products, arithmetic and copies ran while one was open for 2% of the time, Pallas kernels for 0%

commit v1 on v0

--- a/solution.py
+++ b/solution.py
@@ -81,7 +81,7 @@
         lax.all_gather(new_query.astype(jnp.bfloat16), "replica", axis=0, tiled=True),
         lax.all_gather(new_key.astype(jnp.bfloat16), "replica", axis=0, tiled=True),
         lax.all_gather(new_value.astype(jnp.bfloat16), "replica", axis=0, tiled=True),
-        lax.all_gather(new_mixed.astype(jnp.bfloat16), "replica", axis=1, tiled=True),
+        jnp.concatenate(lax.all_gather(new_mixed.astype(jnp.bfloat16), "replica"), axis=1),
         lax.all_gather(new_norm.astype(jnp.bfloat16), "replica", axis=0, tiled=True),
     )
     return (

time: 210 us -> 210 us (level)
    unnamed x36 -> x35, local copies, waits for them, and re-layouts: 4.75 us -> 4.27 us
where the time goes in v1:
time: 210 us
  blocking collectives  91.6 us (44%)
  waiting for transfers between devices  90.2 us (43%)
  between operations  13.9 us (7%)
  other arithmetic  8.91 us (4%)
  local copies, waits for them, and re-layouts  5.13 us (2%)
    reduce_scatter x1, waiting for transfers between devices, local(): lax.psum_scatter(grad_query[0], 'replica', scatter_dimension=0, tiled=True)  27.1 us
    reduce_scatter x1, waiting for transfers between devices, local(): lax.psum_scatter(grad_mixed[0], 'replica', scatter_dimension=1, tiled=True)  27.1 us
    reduce_scatter x1, waiting for transfers between devices, local(): lax.psum_scatter(grad_key[0], 'replica', scatter_dimension=0, tiled=True)  26.9 us
    all_gather x1, blocking collectives, local(): lax.all_gather(new_value.astype(jnp.bfloat16), 'replica', axis=0, tiled=T...  15.5 us
    all_gather x1, blocking collectives, local(): lax.all_gather(new_mixed.astype(jnp.bfloat16), 'replica')  15.3 us
    all_gather x1, blocking collectives, local(): lax.all_gather(new_key.astype(jnp.bfloat16), 'replica', axis=0, tiled=True)  14.8 us
    all_gather x1, blocking collectives, local(): lax.all_gather(new_query.astype(jnp.bfloat16), 'replica', axis=0, tiled=T...  14.8 us
    psum x1, blocking collectives, local(): whole_norm = lax.psum(grad_norm[0], 'replica')  13.5 us
  transfers between devices with their start and end apart: 4, of which 4 were waited for; matrix products, arithmetic and copies ran while one was open for 2% of the time, Pallas kernels for 0%

profile of v1, /device:TPU:0, one launch (start us, length us, event | category | flops | bytes accessed | tf_op | source)
XLA Modules:
  0.0 209.9 jit_solution(17767544554464997413)
XLA Ops:
  10.1 13.5 %psum.71 = f32[1024]{0:T(1024)S(1)} all-reduce(f32[1024]{0:T(1024)S(1)} %bitcast.43), channel_id=1, replica_groups=mesh['job'=2,'replica'=4,'model'=4] {'replica'}, use_global_device_ids=true, to_apply=%region_20.0 | all-reduce | flops 1024 | bytes 8192 | tf_op jit(solution)/shard_map/psum | solution.py:33
  24.3 7.7 %all-gather.1 = bf16[4,1,256]{2,1,0:T(2,128)(2,1)S(1)} all-gather(bf16[1,1,256]{2,1,0:T(2,128)(2,1)S(1)} %reshape.47), channel_id=1, replica_groups=mesh['job'=2,'replica'=4,'model'=4] {'replica'}, dimensions={0}, use_global_device_ids=true | all-gather | bytes 2560 | tf_op jit(solution)/shard_map/all_gather | solution.py:85
  32.8 0.8 copy-done
  33.8 6.6 %reduce-scatter.9.cloned.1.call-done = f32[256,256]{1,0:T(8,128)} async-done(((f32[1024,256]{1,0:T(8,128)}), f32[256,256]{1,0:T(8,128)}) %reduce-scatter.9.cloned.1.call-update) | async-done | bytes 262160 | tf_op jit(solution)/shard_map/reduce_scatter | solution.py:30
  40.4 1.1 multiply_reduce_fusion.2
  41.5 27.1 %reduce-scatter.11.cloned.1.call-done = f32[256,256]{1,0:T(8,128)} async-done(((f32[256,1024]{1,0:T(8,128)}), f32[256,256]{1,0:T(8,128)}) %reduce-scatter.11.cloned.1.call-update) | async-done | bytes 262160 | tf_op jit(solution)/shard_map/reduce_scatter | solution.py:31
  68.6 1.0 multiply_reduce_fusion
  69.6 27.1 %reduce-scatter.5.cloned.1.call-done = f32[256,256]{1,0:T(8,128)} async-done(((f32[1024,256]{1,0:T(8,128)}), f32[256,256]{1,0:T(8,128)}) %reduce-scatter.5.cloned.1.call-update) | async-done | bytes 262160 | tf_op jit(solution)/shard_map/reduce_scatter | solution.py:28
  96.7 1.1 multiply_reduce_fusion.6
  97.7 26.9 %reduce-scatter.7.cloned.1.call-done = f32[256,256]{1,0:T(8,128)} async-done(((f32[1024,256]{1,0:T(8,128)}), f32[256,256]{1,0:T(8,128)}) %reduce-scatter.7.cloned.1.call-update) | async-done | bytes 262160 | tf_op jit(solution)/shard_map/reduce_scatter | solution.py:29
  124.7 1.1 multiply_reduce_fusion.4
  125.8 10.0 %all-reduce = (f32[256,1]{0,1:T(1,128)S(1)}, f32[256,1]{0,1:T(1,128)S(1)}, f32[256,1]{0,1:T(1,128)S(1)}, f32[256,1]{0,1:T(1,128)S(1)}, f32[256,1]{0,1:T(1,128)S(...) all-reduce(f32[256,1]{0,1:T(1,128)S(1)} %bitcast.41, ...), channel_id=1, replica_groups=mesh['job'=2,'replica'=4,'model'=4] {'model'}, use_global_device_ids=true, to_apply=%region_4.0 | all-reduce | flops 2048 | bytes 16384 | tf_op jit(solution)/shard_map/psum | solution.py:53
  135.8 0.9 fusion.3
  136.7 14.8 %all_gather.19 = bf16[1024,256]{1,0:T(8,128)(2,1)S(1)} all-gather(bf16[256,256]{1,0:T(8,128)(2,1)S(1)} %get-tuple-element.32), channel_id=1, replica_groups=mesh['job'=2,'replica'=4,'model'=4] {'replica'}, dimensions={0}, use_global_device_ids=true | all-gather | bytes 655360 | tf_op jit(solution)/shard_map/all_gather | solution.py:82
  151.5 0.9 fusion.2
  152.4 15.5 %all_gather.20 = bf16[1024,256]{1,0:T(8,128)(2,1)S(1)} all-gather(bf16[256,256]{1,0:T(8,128)(2,1)S(1)} %get-tuple-element.29), channel_id=1, replica_groups=mesh['job'=2,'replica'=4,'model'=4] {'replica'}, dimensions={0}, use_global_device_ids=true | all-gather | bytes 655360 | tf_op jit(solution)/shard_map/all_gather | solution.py:83
  168.0 0.8 fusion.1
  168.9 15.3 %all-gather = bf16[1024,256]{1,0:T(8,128)(2,1)S(1)} all-gather(bf16[256,256]{1,0:T(8,128)(2,1)S(1)} %get-tuple-element.26), channel_id=2, replica_groups=mesh['job'=2,'replica'=4,'model'=4] {'replica'}, dimensions={0}, use_global_device_ids=true | all-gather | bytes 655360 | tf_op jit(solution)/shard_map/all_gather | solution.py:84
  184.2 0.9 copy.33
  185.4 0.9 fusion.4
  186.3 14.8 %all_gather.18 = bf16[1024,256]{1,0:T(8,128)(2,1)S(1)} all-gather(bf16[256,256]{1,0:T(8,128)(2,1)S(1)} %get-tuple-element.35), channel_id=1, replica_groups=mesh['job'=2,'replica'=4,'model'=4] {'replica'}, dimensions={0}, use_global_device_ids=true | all-gather | bytes 655360 | tf_op jit(solution)/shard_map/all_gather | solution.py:81
  201.0 0.8 copy.38
  201.8 0.8 copy.39
  202.6 0.8 copy.40
  (48 shorter events, 4.9 us)
Async XLA Ops:
  7.2 33.2 %reduce-scatter.9.cloned.1.call-start = ((), (), s32[]{:S(2)}) async-start(), calls=%async_computation.6 | async-start | bytes 1310720 | tf_op jit(solution)/shard_map/reduce_scatter | solution.py:30
  7.9 60.6 %reduce-scatter.11.cloned.1.call-start = ((), (), s32[]{:S(2)}) async-start(), calls=%async_computation.7 | async-start | bytes 1310720 | tf_op jit(solution)/shard_map/reduce_scatter | solution.py:31
  8.7 88.0 %reduce-scatter.5.cloned.1.call-start = ((), (), s32[]{:S(2)}) async-start(), calls=%async_computation.4 | async-start | bytes 1310720 | tf_op jit(solution)/shard_map/reduce_scatter | solution.py:28
  9.4 115.2 %reduce-scatter.7.cloned.1.call-start = ((), (), s32[]{:S(2)}) async-start(), calls=%async_computation.5 | async-start | bytes 1310720 | tf_op jit(solution)/shard_map/reduce_scatter | solution.py:29
  9.4 0.7 copy-start.12
  9.5 14.1 %copy-start.13 = (f32[256]{0:T(256)S(1)}, f32[256]{0:T(256)}, u32[]{:S(2)}) copy-start(f32[256]{0:T(256)} %param.24) | copy-start | bytes 3076
  9.5 14.1 %copy-start.14 = (f32[256]{0:T(256)S(1)}, f32[256]{0:T(256)}, u32[]{:S(2)}) copy-start(f32[256]{0:T(256)} %param.29) | copy-start | bytes 3076
  9.5 23.1 %copy-start.3 = (f32[256,256]{1,0:T(8,128)S(1)}, f32[256,256]{1,0:T(8,128)}, u32[]{:S(2)}) copy-start(f32[256,256]{1,0:T(8,128)} %param.20) | copy-start | bytes 786436
  10.0 22.7 %copy-start.2 = (f32[256,256]{1,0:T(8,128)S(1)}, f32[256,256]{1,0:T(8,128)}, u32[]{:S(2)}) copy-start(f32[256,256]{1,0:T(8,128)} %param.23) | copy-start | bytes 786436
  32.6 1.0 copy-start
  32.7 1.0 copy-start.1
  69.6 66.2 %copy-start.8 = (f32[256,256]{1,0:T(8,128)S(1)}, f32[256,256]{1,0:T(8,128)}, u32[]{:S(2)}) copy-start(f32[256,256]{1,0:T(8,128)} %param.26) | copy-start | bytes 786436
  124.7 11.2 %copy-start.7 = (f32[256,256]{1,0:T(8,128)S(1)}, f32[256,256]{1,0:T(8,128)}, u32[]{:S(2)}) copy-start(f32[256,256]{1,0:T(8,128)} %reduce-scatter.7.cloned.1.call-done) | copy-start | bytes 786436
  136.7 14.8 %copy-start.6 = (f32[256,256]{1,0:T(8,128)S(1)}, f32[256,256]{1,0:T(8,128)}, u32[]{:S(2)}) copy-start(f32[256,256]{1,0:T(8,128)} %reduce-scatter.9.cloned.1.call-done) | copy-start | bytes 786436
  136.7 14.8 %copy-start.9 = (f32[256,256]{1,0:T(8,128)S(1)}, f32[256,256]{1,0:T(8,128)}, u32[]{:S(2)}) copy-start(f32[256,256]{1,0:T(8,128)} %param.27) | copy-start | bytes 786436
  152.4 15.6 %copy-start.5 = (f32[256,256]{1,0:T(8,128)S(1)}, f32[256,256]{1,0:T(8,128)}, u32[]{:S(2)}) copy-start(f32[256,256]{1,0:T(8,128)} %reduce-scatter.11.cloned.1.call-done) | copy-start | bytes 786436
  152.4 15.6 %copy-start.10 = (f32[256,256]{1,0:T(8,128)S(1)}, f32[256,256]{1,0:T(8,128)}, u32[]{:S(2)}) copy-start(f32[256,256]{1,0:T(8,128)} %param.28) | copy-start | bytes 786436
  184.2 1.0 copy-start.4
  184.2 1.2 copy-start.11
Sparse Core Ops, SparseCore 0:
  10.3 30.1 reduce-scatter.8
  42.7 25.7 reduce-scatter.10
  70.9 25.7 reduce-scatter.4
  98.8 25.7 reduce-scatter.6
